TPU v7x, 32 devices: a whole 2x2x4 slice. The times are simulated.
32 devices in a mesh: row: 16 (over z, x, core), col: 2 (over y).
Axes of the slice: x: 2, y: 2, z: 4, core: 2. Of those that a mesh axis runs over, the one named last changes fastest.
Arguments:
- occupied_waves: bfloat16 [1024, 32768], P('row', 'col'), may hold values from -6 to 6
- virtual_waves: bfloat16 [512, 32768], P('row', 'col'), may hold values from -6 to 6
- occupied_decay: float32 [1024], replicated, may hold values from 0.02 to 1
- virtual_decay: float32 [512], replicated, may hold values from 0.02 to 1
Outputs:
- spectrum_real: float32 [512, 32, 1024], P('row', 'col')
- spectrum_imaginary: float32 [512, 32, 1024], P('row', 'col')
All inputs are finite; a program needn't handle non-finite values.
Results may differ from a plain program's by a relative error of at most 0.0041.
Values may be sent and summed in bfloat16 or wider, within the bound.
A program may use at most 128 MiB of HBM per device.

v0:
```python
import math
import jax
import jax.numpy as jnp
from jax import lax
from jax.sharding import PartitionSpec as P

NOCC = 1024
NVIR = 512
NA = 32
NB = 32
NC = 32
ROWS_DEV = 32
NGRID = 32768


def tables(length):
    index = jnp.arange(length, dtype=jnp.int32)
    phase = index[:, None] * index[None, :] % length
    angle = phase.astype(jnp.float32) * (2.0 * math.pi / length)
    return (jnp.cos(angle), jnp.sin(angle))


def apply_table(form, data, table):
    return jnp.einsum(form, data, table, precision=lax.Precision.HIGHEST)


def real_step(data, form, length):
    cosine, sine = tables(length)
    return (apply_table(form, data, cosine), -apply_table(form, data, sine))


def complex_step(real_part, imag_part, form, length):
    cosine, sine = tables(length)
    new_real = apply_table(form, real_part, cosine) + apply_table(form, imag_part, sine)
    new_imag = apply_table(form, imag_part, cosine) - apply_table(form, real_part, sine)
    return (new_real, new_imag)


def scale_rows(waves, decay):
    return (waves * decay[:, None]).astype(jnp.bfloat16)


def place(waves, window, start_col):
    block_cols = waves.shape[1]
    buffer = jnp.zeros((waves.shape[0], window + block_cols), jnp.bfloat16)
    buffer = lax.dynamic_update_slice(buffer, waves, (jnp.int32(0), start_col))
    return buffer[:, :window]


def on_device(occupied_waves, virtual_waves, occupied_decay, virtual_decay):
    block_cols = occupied_waves.shape[1]
    row_count = lax.axis_size("row")
    contract = (((0,), (0,)), ((), ()))
    factor = -1.0 / math.sqrt(NOCC * NVIR)
    window = ROWS_DEV * row_count
    start_col = lax.axis_index("col") * block_cols
    plane_cols = NB * NC
    per_col = block_cols // plane_cols
    spread = row_count // per_col
    sub_rows = ROWS_DEV // spread

    def spread_planes(waves):
        share = waves.shape[0]
        shaped = waves.reshape(share, per_col, 1, plane_cols)
        shaped = jnp.broadcast_to(shaped, (share, per_col, spread, plane_cols))
        return shaped.reshape(share, row_count * plane_cols)

    def pick_rows(waves):
        share = waves.shape[0]
        shaped = place(waves, window, start_col).reshape(share, row_count, spread, sub_rows)
        shaped = jnp.transpose(shaped, (0, 2, 1, 3))[:, None]
        shaped = jnp.broadcast_to(shaped, (share, per_col, spread, row_count, sub_rows))
        return shaped.reshape(share, row_count * row_count * sub_rows)

    plane_occ, plane_vir = (
        lax.all_to_all(
            spread_planes(occupied_waves), "row", split_axis=1, concat_axis=0, tiled=True
        ),
        lax.all_to_all(
            spread_planes(virtual_waves), "row", split_axis=1, concat_axis=0, tiled=True
        ),
    )
    part_occ, part_vir = (
        lax.all_to_all(pick_rows(occupied_waves), "row", split_axis=1, concat_axis=0, tiled=True),
        lax.all_to_all(pick_rows(virtual_waves), "row", split_axis=1, concat_axis=0, tiled=True),
    )
    occ_rows, vir_rows = (
        lax.psum(part_occ.astype(jnp.float32).astype(jnp.bfloat16), "col").astype(jnp.float32),
        lax.psum(part_vir.astype(jnp.float32).astype(jnp.bfloat16), "col").astype(jnp.float32),
    )
    occ_rows = scale_rows(occ_rows, occupied_decay)
    vir_rows = scale_rows(vir_rows, virtual_decay)
    green_occ = lax.dot_general(plane_occ, occ_rows, contract, preferred_element_type=jnp.float32)
    green_vir = lax.dot_general(plane_vir, vir_rows, contract, preferred_element_type=jnp.float32)
    polar = green_occ * green_vir * factor
    cube = polar.reshape(1, NB, NC, row_count * sub_rows)
    real_part, imag_part = real_step(cube, "abcr,cw->wabr", NC)
    real_part, imag_part = complex_step(real_part, imag_part, "wabr,bv->wavr", NB)
    blocked = (NC, 1, NB, row_count, sub_rows)
    real_part, imag_part = (
        lax.all_to_all(
            lax.all_to_all(
                real_part.reshape(blocked), "row", split_axis=3, concat_axis=3, tiled=True
            ),
            "col",
            split_axis=0,
            concat_axis=1,
            tiled=True,
        ),
        lax.all_to_all(
            lax.all_to_all(
                imag_part.reshape(blocked), "row", split_axis=3, concat_axis=3, tiled=True
            ),
            "col",
            split_axis=0,
            concat_axis=1,
            tiled=True,
        ),
    )

    def settle(part):
        kc_share = part.shape[0]
        part = part.reshape(kc_share, part.shape[1], NB, per_col, spread, sub_rows)
        part = jnp.transpose(part, (0, 1, 3, 2, 4, 5))
        return part.reshape(kc_share, NA, NB, ROWS_DEV)

    real_part, imag_part = complex_step(settle(real_part), settle(imag_part), "wavr,au->rwuv", NA)
    normal = 1.0 / math.sqrt(NGRID)
    final_shape = (real_part.shape[0], real_part.shape[1], NA * NB)
    return ((real_part * normal).reshape(final_shape), (imag_part * normal).reshape(final_shape))


def solution(mesh):
    in_specs = (P("row", "col"), P("row", "col"), P(), P())
    out_specs = (P("row", "col", None), P("row", "col", None))
    return jax.shard_map(
        on_device, mesh=mesh, in_specs=in_specs, out_specs=out_specs, check_vma=False
    )
```

profile of v0, /device:TPU:10, one launch (start us, length us, event | category | flops | bytes accessed | tf_op | source)
XLA Modules:
  0.0 507.3 jit_solution(10017124884010591523)
XLA Ops:
  16.1 12.9 %all-to-all-done.2 = bf16[32,16,512]{2,0,1:T(8,128)(2,1)S(1)} async-done(((bf16[32,16,512]{2,0,1:T(8,128)(2,1)}), bf16[32,16,512]{2,0,1:T(8,128)(2,1)S(1)}, u32[]{:S(2)}, u32[]{:S(2)}) %all-to-all-start.2) | async-done | bytes 524320 | tf_op jit(solution)/shard_map/all_to_all | solution.py:85
  36.8 23.0 %all-to-all-done = bf16[64,16,512]{2,0,1:T(8,128)(2,1)S(1)} async-done(((bf16[64,16,512]{2,0,1:T(8,128)(2,1)}), bf16[64,16,512]{2,0,1:T(8,128)(2,1)S(1)}, u32[]{:S(2)}, u32[]{:S(2)}) %all-to-all-start) | async-done | bytes 1048608 | tf_op jit(solution)/shard_map/all_to_all | solution.py:84
  67.1 46.1 %all-to-all-done.1 = bf16[64,16,1024]{2,0,1:T(8,128)(2,1)S(1)} async-done(((bf16[64,16,1024]{2,0,1:T(8,128)(2,1)}), bf16[64,16,1024]{2,0,1:T(8,128)(2,1)S(1)}, u32[]{:S(2)}, u32[]{:S(2)}) %all-to-all-start.1) | async-done | bytes 2097184 | tf_op jit(solution)/shard_map/all_to_all | solution.py:76
  119.0 55.5 %all-reduce.3.cloned.1.call-done = (bf16[1024,512]{1,0:T(8,128)(2,1)}, bf16[512,512]{1,0:T(8,128)(2,1)}) async-done(((bf16[1024,512]{1,0:T(8,128)(2,1)}, bf16[512,512]{1,0:T(8,128)(2,1)}), (bf16[1024,512]{1,0:T(8,128)(2,1)}, bf16[512,512]{1,0:T(8,128)(2,1)})) %all-reduce.3.cloned.1.call-update) | async-done | bytes 1572880 | tf_op jit(solution)/shard_map/psum | solution.py:88
  205.8 9.3 %copy.71 = f32[32,1,32,16,32]{4,2,0,1,3:T(8,128)} copy(f32[32,1,32,16,32]{4,3,2,0,1:T(8,128)} %reshape.86) | data formatting | bytes 4194304 | tf_op jit(solution)/shard_map/reshape | solution.py:112
  215.1 8.6 %reshape.99 = f32[16,1,32768]{2,1,0:T(1,128)} reshape(f32[16,1,32,32,32]{4,3,2,1,0:T(8,128)} %bitcast.113) | data formatting | bytes 4194304
  244.9 9.3 %copy.72 = f32[32,1,32,16,32]{4,2,0,1,3:T(8,128)} copy(f32[32,1,32,16,32]{4,3,2,0,1:T(8,128)} %reshape.83) | data formatting | bytes 4194304 | tf_op jit(solution)/shard_map/reshape | solution.py:103
  254.2 8.6 %reshape.95 = f32[16,1,32768]{2,1,0:T(1,128)} reshape(f32[16,1,32,32,32]{4,3,2,1,0:T(8,128)} %bitcast.114) | data formatting | bytes 4194304
  262.7 14.2 %all-to-all-done.6 = f32[16,1,32768]{2,1,0:T(1,128)} async-done(((f32[16,1,32768]{2,1,0:T(1,128)}), f32[16,1,32768]{2,1,0:T(1,128)}, u32[]{:S(2)}, u32[]{:S(2)}) %all-to-all-start.6) | async-done | bytes 2097184 | tf_op jit(solution)/shard_map/all_to_all | solution.py:111
  295.4 14.2 %copy.45 = f32[32,1,32,16,32]{4,3,2,1,0:T(8,128)} copy(f32[32,1,32,16,32]{4,2,0,1,3:T(8,128)} %bitcast.115) | data formatting | bytes 4194304 | tf_op jit(solution)/shard_map/all_to_all | solution.py:111
  316.4 13.3 %all-to-all-done.4 = f32[16,1,32768]{2,1,0:T(1,128)} async-done(((f32[16,1,32768]{2,1,0:T(1,128)}), f32[16,1,32768]{2,1,0:T(1,128)}, u32[]{:S(2)}, u32[]{:S(2)}) %all-to-all-start.4) | async-done | bytes 2097184 | tf_op jit(solution)/shard_map/all_to_all | solution.py:102
  334.7 7.3 %reduce = f32[16,32768]{1,0:T(8,128)S(1)} reduce(f32[16,1,32768]{2,1,0:T(1,128)} %all-to-all-done.4, f32[]{:T(128)} %broadcast.102), dimensions={1}, to_apply=%all_to_all.94.reduce_sub_computation | reduce | bytes 4194308 | tf_op jit(solution)/shard_map/all_to_all | solution.py:102
  346.7 14.2 %copy.40 = f32[32,1,32,16,32]{4,3,2,1,0:T(8,128)} copy(f32[32,1,32,16,32]{4,2,0,1,3:T(8,128)} %bitcast.116) | data formatting | bytes 4194304 | tf_op jit(solution)/shard_map/all_to_all | solution.py:102
  372.6 8.5 %reduce.3 = f32[2,262144]{1,0:T(2,128)S(1)} reduce(f32[2,1,262144]{2,1,0:T(1,128)} %all-to-all-done.7, f32[]{:T(128)} %broadcast.102), dimensions={1}, to_apply=%all_to_all.99.reduce_sub_computation | reduce | bytes 4194308 | tf_op jit(solution)/shard_map/all_to_all | solution.py:110
  387.5 7.7 %copy.46 = f32[2,16,1,32,16,32]{5,4,0,3,1,2:T(8,128)} copy(f32[2,16,1,32,16,32]{5,4,3,1,0,2:T(8,128)} %bitcast.117) | data formatting | bytes 4194304 | tf_op jit(solution)/shard_map/all_to_all | solution.py:110
  398.3 8.2 %reduce.1 = f32[2,262144]{1,0:T(2,128)S(1)} reduce(f32[2,1,262144]{2,1,0:T(1,128)} %all-to-all-done.5, f32[]{:T(128)} %broadcast.102), dimensions={1}, to_apply=%all_to_all.95.reduce_sub_computation | reduce | bytes 4194308 | tf_op jit(solution)/shard_map/all_to_all | solution.py:101
  417.6 9.5 %fusion.22 = f32[32,16,32,32]{3,0,2,1:T(8,128)} fusion(f32[16,32,32,32]{3,1,2,0:T(8,128)S(1)} %bitcast.111), kind=kOutput, calls=%fused_computation.31 | convolution fusion | flops 201340928 | bytes 4194304 | tf_op jit(solution)/shard_map/wavr,au->rwuv/dot_general | solution.py:24
  427.1 9.8 %fusion.20 = f32[32,16,32,32]{3,0,2,1:T(8,128)} fusion(f32[16,32,32,32]{3,1,2,0:T(8,128)S(1)} %bitcast.109), kind=kOutput, calls=%fused_computation.29 | convolution fusion | flops 201340928 | bytes 4194304 | tf_op jit(solution)/shard_map/wavr,au->rwuv/dot_general | solution.py:24
  436.9 12.1 %multiply_bitcast_fusion.1 = f32[32,16,32,32]{0,2,3,1:T(8,128)} fusion(f32[32,16,32,32]{3,0,2,1:T(8,128)} %fusion.22, f32[16,32,32,32]{3,1,2,0:T(8,128)S(1)} %bitcast.110), kind=kOutput, calls=%fused_computation.1 | convolution fusion | flops 202389504 | bytes 6291456 | tf_op jit(solution)/shard_map/wavr,au->rwuv/dot_general | solution.py:24
  449.0 12.4 %multiply_bitcast_fusion = f32[32,16,32,32]{0,2,3,1:T(8,128)} fusion(f32[32,16,32,32]{3,0,2,1:T(8,128)} %fusion.20, f32[16,32,32,32]{3,1,2,0:T(8,128)S(1)} %bitcast.112), kind=kOutput, calls=%fused_computation | convolution fusion | flops 202389504 | bytes 6291456 | tf_op jit(solution)/shard_map/wavr,au->rwuv/dot_general | solution.py:24
  461.4 11.7 %copy.48 = f32[32,16,32,32]{3,2,1,0:T(8,128)} copy(f32[32,16,32,32]{0,2,3,1:T(8,128)} %multiply_bitcast_fusion) | data formatting | bytes 4194304 | tf_op jit(solution)/shard_map/mul | solution.py:130
  473.1 7.7 %reshape.90 = f32[32,16,1024]{2,1,0:T(8,128)} reshape(f32[32,16,32,32]{3,2,1,0:T(8,128)} %copy.48) | data formatting | bytes 4194304 | tf_op jit(solution)/shard_map/reshape | solution.py:130
  480.8 11.7 %copy.47 = f32[32,16,32,32]{3,2,1,0:T(8,128)} copy(f32[32,16,32,32]{0,2,3,1:T(8,128)} %multiply_bitcast_fusion.1) | data formatting | bytes 4194304 | tf_op jit(solution)/shard_map/mul | solution.py:130
  492.5 7.7 %reshape.89 = f32[32,16,1024]{2,1,0:T(8,128)} reshape(f32[32,16,32,32]{3,2,1,0:T(8,128)} %copy.47) | data formatting | bytes 4194304 | tf_op jit(solution)/shard_map/reshape | solution.py:130
  (64 shorter events, 149.4 us)
Async XLA Ops:
  8.6 7.3 %copy-start.2 = (bf16[64,16384]{1,0:T(8,128)(2,1)S(1)}, bf16[64,16384]{1,0:T(8,128)(2,1)}, u32[]{:S(2)}) copy-start(bf16[64,16384]{1,0:T(8,128)(2,1)} %param.4) | copy-start | bytes 6291460
  9.4 19.5 %all-to-all-start.2 = ((bf16[32,16,512]{2,0,1:T(8,128)(2,1)}), bf16[32,16,512]{2,0,1:T(8,128)(2,1)S(1)}, u32[]{:S(2)}, u32[]{:S(2)}) async-start(bf16[32,16,512]{2,0,1:T(8,128)(2,1)} %broadcast_in_dim.11), calls=%async_computation.2 | async-start | bytes 1048576 | tf_op jit(solution)/shard_map/all_to_all | solution.py:85
  29.0 1.1 copy-start.5
  30.1 29.7 %all-to-all-start = ((bf16[64,16,512]{2,0,1:T(8,128)(2,1)}), bf16[64,16,512]{2,0,1:T(8,128)(2,1)S(1)}, u32[]{:S(2)}, u32[]{:S(2)}) async-start(bf16[64,16,512]{2,0,1:T(8,128)(2,1)} %broadcast_in_dim.9), calls=%async_computation | async-start | bytes 2097152 | tf_op jit(solution)/shard_map/all_to_all | solution.py:84
  59.9 1.0 copy-start.4
  60.8 5.2 %copy-start.3 = (bf16[32,16384]{1,0:T(8,128)(2,1)S(1)}, bf16[32,16384]{1,0:T(8,128)(2,1)}, u32[]{:S(2)}) copy-start(bf16[32,16384]{1,0:T(8,128)(2,1)} %param.5) | copy-start | bytes 3145732
  60.8 52.4 %all-to-all-start.1 = ((bf16[64,16,1024]{2,0,1:T(8,128)(2,1)}), bf16[64,16,1024]{2,0,1:T(8,128)(2,1)S(1)}, u32[]{:S(2)}, u32[]{:S(2)}) async-start(bf16[64,16,1024]{2,0,1:T(8,128)(2,1)} %bitcast.123), calls=%async_computation.1 | async-start | bytes 4194304 | tf_op jit(solution)/shard_map/all_to_all | solution.py:76
  67.1 107.4 %copy-start.6 = (f32[1024]{0:T(1024)S(1)}, f32[1024]{0:T(1024)}, u32[]{:S(2)}) copy-start(f32[1024]{0:T(1024)} %param.6) | copy-start | bytes 12292
  113.2 65.3 %all-to-all-start.3 = ((bf16[32,16,1024]{2,0,1:T(8,128)(2,1)}), bf16[32,16,1024]{2,0,1:T(8,128)(2,1)S(1)}, u32[]{:S(2)}, u32[]{:S(2)}) async-start(bf16[32,16,1024]{2,0,1:T(8,128)(2,1)} %bitcast.126), calls=%async_computation.3 | async-start | bytes 2097152 | tf_op jit(solution)/shard_map/all_to_all | solution.py:79
  118.3 56.3 %all-reduce.3.cloned.1.call-start = ((), (), s32[]{:S(2)}) async-start(), calls=%async_computation.8 | async-start | bytes 3145728 | tf_op jit(solution)/shard_map/psum | solution.py:88
  174.5 3.9 copy-start.7
  184.5 1.3 copy-start.1
  187.7 4.3 copy-start
  223.7 53.3 %all-to-all-start.6 = ((f32[16,1,32768]{2,1,0:T(1,128)}), f32[16,1,32768]{2,1,0:T(1,128)}, u32[]{:S(2)}, u32[]{:S(2)}) async-start(f32[16,1,32768]{2,1,0:T(1,128)} %reshape.99), calls=%async_computation.6 | async-start | bytes 4194304 | tf_op jit(solution)/shard_map/all_to_all | solution.py:111
  277.0 52.7 %all-to-all-start.4 = ((f32[16,1,32768]{2,1,0:T(1,128)}), f32[16,1,32768]{2,1,0:T(1,128)}, u32[]{:S(2)}, u32[]{:S(2)}) async-start(f32[16,1,32768]{2,1,0:T(1,128)} %reshape.95), calls=%async_computation.4 | async-start | bytes 4194304 | tf_op jit(solution)/shard_map/all_to_all | solution.py:102
  329.7 38.1 %all-to-all-start.7 = ((f32[2,1,262144]{2,1,0:T(1,128)}), f32[2,1,262144]{2,1,0:T(1,128)}, u32[]{:S(2)}, u32[]{:S(2)}) async-start(f32[2,1,262144]{2,1,0:T(1,128)} %reshape.101), calls=%async_computation.7 | async-start | bytes 4194304 | tf_op jit(solution)/shard_map/all_to_all | solution.py:110
  367.8 30.6 %all-to-all-start.5 = ((f32[2,1,262144]{2,1,0:T(1,128)}), f32[2,1,262144]{2,1,0:T(1,128)}, u32[]{:S(2)}, u32[]{:S(2)}) async-start(f32[2,1,262144]{2,1,0:T(1,128)} %reshape.97), calls=%async_computation.5 | async-start | bytes 4194304 | tf_op jit(solution)/shard_map/all_to_all | solution.py:101
  413.0 14.1 %slice-start = ((s8[8388608]{0:T(1024)(128)(4,1)}), s8[4194304]{0:T(1024)(128)(4,1)S(1)}, s32[]{:S(2)}) async-start(s8[8388608]{0:T(1024)(128)(4,1)} %bitcast.107), calls=%async_computation.9 | async-start | bytes 8388608
  417.6 9.5 %slice-start.1 = ((s8[8388608]{0:T(1024)(128)(4,1)}), s8[4194304]{0:T(1024)(128)(4,1)S(1)}, s32[]{:S(2)}) async-start(s8[8388608]{0:T(1024)(128)(4,1)} %bitcast.107), calls=%async_computation.10 | async-start | bytes 8388608
Sparse Core Ops, SparseCore 0:
  122.0 52.4 all-reduce.2
where the time goes:
time: 513 us; the launch traced here: 507 us
  local copies, waits for them, and re-layouts  175 us (34%)
  waiting for transfers between devices  169 us (33%)
  matrix products  74.2 us (14%)
  starting transfers between devices  43.2 us (8%)
  other arithmetic  31.2 us (6%)
  between operations  14.5 us (3%)
    dot_general x10, matrix products, apply_table(): return jnp.einsum(form, data, table, precision=lax.Precision.HIGHEST)  66.3 us
    unnamed x28, local copies, waits for them, and re-layouts  55.6 us
    psum x1, waiting for transfers between devices, on_device(): lax.psum(part_occ.astype(jnp.float32).astype(jnp.bfloat16), 'col')  55.5 us
    all_to_all x1, waiting for transfers between devices, on_device(): lax.all_to_all(spread_planes(occupied_waves), 'row', split_axis=1, concat...  46.1 us
    all_to_all x1, waiting for transfers between devices, on_device(): lax.all_to_all(pick_rows(occupied_waves), 'row', split_axis=1, concat_axi...  23 us
    reshape x2, local copies, waits for them, and re-layouts, on_device(): imag_part.reshape(blocked)  15.7 us
    reshape x2, local copies, waits for them, and re-layouts, on_device(): real_part.reshape(blocked)  15.5 us
    all_to_all x2, local copies, waits for them, and re-layouts, on_device(): lax.all_to_all(real_part.reshape(blocked), 'row', split_axis=3, concat_ax...  14.8 us
  transfers between devices with their start and end apart: 9, of which 7 were waited for; matrix products, arithmetic and copies ran while one was open for 26% of the time, Pallas kernels for 0%

commit v1 on v0

--- a/solution.py
+++ b/solution.py
@@ -11,6 +11,11 @@
 NC = 32
 ROWS_DEV = 32
 NGRID = 32768
+
+
+def gather_and_add(x, mesh_axis):
+    parts = lax.all_gather(x, mesh_axis)
+    return jnp.sum(parts, axis=0)
 
 
 def tables(length):
@@ -85,7 +90,9 @@
         lax.all_to_all(pick_rows(virtual_waves), "row", split_axis=1, concat_axis=0, tiled=True),
     )
     occ_rows, vir_rows = (
-        lax.psum(part_occ.astype(jnp.float32).astype(jnp.bfloat16), "col").astype(jnp.float32),
+        gather_and_add(part_occ.astype(jnp.float32).astype(jnp.bfloat16), "col").astype(
+            jnp.float32
+        ),
         lax.psum(part_vir.astype(jnp.float32).astype(jnp.bfloat16), "col").astype(jnp.float32),
     )
     occ_rows = scale_rows(occ_rows, occupied_decay)

time: 513 us -> 487 us (0.949)
  waiting for transfers between devices: 169 us -> 140 us
    psum x1, waiting for transfers between devices: 55.5 us -> 26.6 us  [on_device(): lax.psum(part_vir.astype(jnp.float32).astype(jnp.bfloat16), 'col')]
  transfers between devices with their start and end apart: 9 -> 10, of which waited for: 7 -> 7; matrix products, arithmetic and copies ran while one was open for 26% -> 27% of each run, Pallas kernels for 0% -> 0%
where the time goes in v1:
time: 487 us; the launch traced here: 481 us
  local copies, waits for them, and re-layouts  175 us (36%)
  waiting for transfers between devices  140 us (29%)
  matrix products  73.3 us (15%)
  starting transfers between devices  43.2 us (9%)
  other arithmetic  33.5 us (7%)
  between operations  14.8 us (3%)
    dot_general x10, matrix products, apply_table(): return jnp.einsum(form, data, table, precision=lax.Precision.HIGHEST)  66.4 us
    unnamed x28, local copies, waits for them, and re-layouts  55.7 us
    all_to_all x1, waiting for transfers between devices, on_device(): lax.all_to_all(spread_planes(occupied_waves), 'row', split_axis=1, concat...  45.3 us
    psum x1, waiting for transfers between devices, on_device(): lax.psum(part_vir.astype(jnp.float32).astype(jnp.bfloat16), 'col')  26.6 us
    all_to_all x1, waiting for transfers between devices, on_device(): lax.all_to_all(pick_rows(occupied_waves), 'row', split_axis=1, concat_axi...  23 us
    reshape x2, local copies, waits for them, and re-layouts, on_device(): imag_part.reshape(blocked)  15.9 us
    reshape x2, local copies, waits for them, and re-layouts, on_device(): real_part.reshape(blocked)  15.5 us
    all_to_all x2, local copies, waits for them, and re-layouts, on_device(): lax.all_to_all(real_part.reshape(blocked), 'row', split_axis=3, concat_ax...  14.7 us
  transfers between devices with their start and end apart: 10, of which 7 were waited for; matrix products, arithmetic and copies ran while one was open for 27% of the time, Pallas kernels for 0%

profile of v1, /device:TPU:10, one launch (start us, length us, event | category | flops | bytes accessed | tf_op | source)
XLA Modules:
  0.0 480.5 jit_solution(6654739943282514132)
XLA Ops:
  16.1 12.9 %all-to-all-done.2 = bf16[32,16,512]{2,0,1:T(8,128)(2,1)S(1)} async-done(((bf16[32,16,512]{2,0,1:T(8,128)(2,1)}), bf16[32,16,512]{2,0,1:T(8,128)(2,1)S(1)}, u32[]{:S(2)}, u32[]{:S(2)}) %all-to-all-start.2) | async-done | bytes 524320 | tf_op jit(solution)/shard_map/all_to_all | solution.py:90
  36.8 23.0 %all-to-all-done = bf16[64,16,512]{2,0,1:T(8,128)(2,1)S(1)} async-done(((bf16[64,16,512]{2,0,1:T(8,128)(2,1)}), bf16[64,16,512]{2,0,1:T(8,128)(2,1)S(1)}, u32[]{:S(2)}, u32[]{:S(2)}) %all-to-all-start) | async-done | bytes 1048608 | tf_op jit(solution)/shard_map/all_to_all | solution.py:89
  67.9 45.3 %all-to-all-done.1 = bf16[64,16,1024]{2,0,1:T(8,128)(2,1)S(1)} async-done(((bf16[64,16,1024]{2,0,1:T(8,128)(2,1)}), bf16[64,16,1024]{2,0,1:T(8,128)(2,1)S(1)}, u32[]{:S(2)}, u32[]{:S(2)}) %all-to-all-start.1) | async-done | bytes 2097184 | tf_op jit(solution)/shard_map/all_to_all | solution.py:81
  124.4 26.6 %all-reduce.2.cloned.1.call-done = bf16[512,512]{1,0:T(8,128)(2,1)} async-done(((bf16[512,512]{1,0:T(8,128)(2,1)}), bf16[512,512]{1,0:T(8,128)(2,1)}) %all-reduce.2.cloned.1.call-update) | async-done | bytes 524304 | tf_op jit(solution)/shard_map/psum | solution.py:96
  178.9 9.3 %copy.71 = f32[32,1,32,16,32]{4,2,0,1,3:T(8,128)} copy(f32[32,1,32,16,32]{4,3,2,0,1:T(8,128)} %reshape.87) | data formatting | bytes 4194304 | tf_op jit(solution)/shard_map/reshape | solution.py:119
  188.2 8.6 %reshape.100 = f32[16,1,32768]{2,1,0:T(1,128)} reshape(f32[16,1,32,32,32]{4,3,2,1,0:T(8,128)} %bitcast.113) | data formatting | bytes 4194304
  217.9 9.3 %copy.72 = f32[32,1,32,16,32]{4,2,0,1,3:T(8,128)} copy(f32[32,1,32,16,32]{4,3,2,0,1:T(8,128)} %reshape.84) | data formatting | bytes 4194304 | tf_op jit(solution)/shard_map/reshape | solution.py:110
  227.2 8.6 %reshape.96 = f32[16,1,32768]{2,1,0:T(1,128)} reshape(f32[16,1,32,32,32]{4,3,2,1,0:T(8,128)} %bitcast.114) | data formatting | bytes 4194304
  235.8 14.2 %all-to-all-done.6 = f32[16,1,32768]{2,1,0:T(1,128)} async-done(((f32[16,1,32768]{2,1,0:T(1,128)}), f32[16,1,32768]{2,1,0:T(1,128)}, u32[]{:S(2)}, u32[]{:S(2)}) %all-to-all-start.6) | async-done | bytes 2097184 | tf_op jit(solution)/shard_map/all_to_all | solution.py:118
  268.1 14.2 %copy.45 = f32[32,1,32,16,32]{4,3,2,1,0:T(8,128)} copy(f32[32,1,32,16,32]{4,2,0,1,3:T(8,128)} %bitcast.115) | data formatting | bytes 4194304 | tf_op jit(solution)/shard_map/all_to_all | solution.py:118
  289.2 13.4 %all-to-all-done.4 = f32[16,1,32768]{2,1,0:T(1,128)} async-done(((f32[16,1,32768]{2,1,0:T(1,128)}), f32[16,1,32768]{2,1,0:T(1,128)}, u32[]{:S(2)}, u32[]{:S(2)}) %all-to-all-start.4) | async-done | bytes 2097184 | tf_op jit(solution)/shard_map/all_to_all | solution.py:109
  307.7 7.2 %reduce.1 = f32[16,32768]{1,0:T(8,128)S(1)} reduce(f32[16,1,32768]{2,1,0:T(1,128)} %all-to-all-done.4, f32[]{:T(128)} %broadcast.102), dimensions={1}, to_apply=%all_to_all.91.reduce_sub_computation | reduce | bytes 4194308 | tf_op jit(solution)/shard_map/all_to_all | solution.py:109
  319.7 14.2 %copy.40 = f32[32,1,32,16,32]{4,3,2,1,0:T(8,128)} copy(f32[32,1,32,16,32]{4,2,0,1,3:T(8,128)} %bitcast.116) | data formatting | bytes 4194304 | tf_op jit(solution)/shard_map/all_to_all | solution.py:109
  345.6 8.2 %reduce.4 = f32[2,262144]{1,0:T(2,128)S(1)} reduce(f32[2,1,262144]{2,1,0:T(1,128)} %all-to-all-done.7, f32[]{:T(128)} %broadcast.102), dimensions={1}, to_apply=%all_to_all.96.reduce_sub_computation | reduce | bytes 4194308 | tf_op jit(solution)/shard_map/all_to_all | solution.py:117
  360.2 7.7 %copy.46 = f32[2,16,1,32,16,32]{5,4,0,3,1,2:T(8,128)} copy(f32[2,16,1,32,16,32]{5,4,3,1,0,2:T(8,128)} %bitcast.117) | data formatting | bytes 4194304 | tf_op jit(solution)/shard_map/all_to_all | solution.py:117
  371.3 8.2 %reduce.2 = f32[2,262144]{1,0:T(2,128)S(1)} reduce(f32[2,1,262144]{2,1,0:T(1,128)} %all-to-all-done.5, f32[]{:T(128)} %broadcast.102), dimensions={1}, to_apply=%all_to_all.92.reduce_sub_computation | reduce | bytes 4194308 | tf_op jit(solution)/shard_map/all_to_all | solution.py:108
  390.6 9.5 %fusion.22 = f32[32,16,32,32]{3,0,2,1:T(8,128)} fusion(f32[16,32,32,32]{3,1,2,0:T(8,128)S(1)} %bitcast.111), kind=kOutput, calls=%fused_computation.31 | convolution fusion | flops 201340928 | bytes 4194304 | tf_op jit(solution)/shard_map/wavr,au->rwuv/dot_general | solution.py:29
  400.1 9.8 %fusion.20 = f32[32,16,32,32]{3,0,2,1:T(8,128)} fusion(f32[16,32,32,32]{3,1,2,0:T(8,128)S(1)} %bitcast.109), kind=kOutput, calls=%fused_computation.29 | convolution fusion | flops 201340928 | bytes 4194304 | tf_op jit(solution)/shard_map/wavr,au->rwuv/dot_general | solution.py:29
  409.9 12.1 %multiply_bitcast_fusion.1 = f32[32,16,32,32]{0,2,3,1:T(8,128)} fusion(f32[32,16,32,32]{3,0,2,1:T(8,128)} %fusion.22, f32[16,32,32,32]{3,1,2,0:T(8,128)S(1)} %bitcast.110), kind=kOutput, calls=%fused_computation.1 | convolution fusion | flops 202389504 | bytes 6291456 | tf_op jit(solution)/shard_map/wavr,au->rwuv/dot_general | solution.py:29
  422.0 12.4 %multiply_bitcast_fusion = f32[32,16,32,32]{0,2,3,1:T(8,128)} fusion(f32[32,16,32,32]{3,0,2,1:T(8,128)} %fusion.20, f32[16,32,32,32]{3,1,2,0:T(8,128)S(1)} %bitcast.112), kind=kOutput, calls=%fused_computation | convolution fusion | flops 202389504 | bytes 6291456 | tf_op jit(solution)/shard_map/wavr,au->rwuv/dot_general | solution.py:29
  434.5 11.6 %copy.48 = f32[32,16,32,32]{3,2,1,0:T(8,128)} copy(f32[32,16,32,32]{0,2,3,1:T(8,128)} %multiply_bitcast_fusion) | data formatting | bytes 4194304 | tf_op jit(solution)/shard_map/mul | solution.py:137
  446.1 7.7 %reshape.91 = f32[32,16,1024]{2,1,0:T(8,128)} reshape(f32[32,16,32,32]{3,2,1,0:T(8,128)} %copy.48) | data formatting | bytes 4194304 | tf_op jit(solution)/shard_map/reshape | solution.py:137
  453.8 11.6 %copy.47 = f32[32,16,32,32]{3,2,1,0:T(8,128)} copy(f32[32,16,32,32]{0,2,3,1:T(8,128)} %multiply_bitcast_fusion.1) | data formatting | bytes 4194304 | tf_op jit(solution)/shard_map/mul | solution.py:137
  465.5 7.7 %reshape.90 = f32[32,16,1024]{2,1,0:T(8,128)} reshape(f32[32,16,32,32]{3,2,1,0:T(8,128)} %copy.47) | data formatting | bytes 4194304 | tf_op jit(solution)/shard_map/reshape | solution.py:137
  (68 shorter events, 152.2 us)
Async XLA Ops:
  8.6 7.3 %copy-start.2 = (bf16[64,16384]{1,0:T(8,128)(2,1)S(1)}, bf16[64,16384]{1,0:T(8,128)(2,1)}, u32[]{:S(2)}) copy-start(bf16[64,16384]{1,0:T(8,128)(2,1)} %param.4) | copy-start | bytes 6291460
  9.4 19.5 %all-to-all-start.2 = ((bf16[32,16,512]{2,0,1:T(8,128)(2,1)}), bf16[32,16,512]{2,0,1:T(8,128)(2,1)S(1)}, u32[]{:S(2)}, u32[]{:S(2)}) async-start(bf16[32,16,512]{2,0,1:T(8,128)(2,1)} %broadcast_in_dim.11), calls=%async_computation.2 | async-start | bytes 1048576 | tf_op jit(solution)/shard_map/all_to_all | solution.py:90
  29.0 1.1 copy-start.5
  30.1 29.7 %all-to-all-start = ((bf16[64,16,512]{2,0,1:T(8,128)(2,1)}), bf16[64,16,512]{2,0,1:T(8,128)(2,1)S(1)}, u32[]{:S(2)}, u32[]{:S(2)}) async-start(bf16[64,16,512]{2,0,1:T(8,128)(2,1)} %broadcast_in_dim.9), calls=%async_computation | async-start | bytes 2097152 | tf_op jit(solution)/shard_map/all_to_all | solution.py:89
  59.9 1.0 copy-start.4
  60.8 6.0 %copy-start.3 = (bf16[32,16384]{1,0:T(8,128)(2,1)S(1)}, bf16[32,16384]{1,0:T(8,128)(2,1)}, u32[]{:S(2)}) copy-start(bf16[32,16384]{1,0:T(8,128)(2,1)} %param.5) | copy-start | bytes 3145732
  60.8 52.4 %all-to-all-start.1 = ((bf16[64,16,1024]{2,0,1:T(8,128)(2,1)}), bf16[64,16,1024]{2,0,1:T(8,128)(2,1)S(1)}, u32[]{:S(2)}, u32[]{:S(2)}) async-start(bf16[64,16,1024]{2,0,1:T(8,128)(2,1)} %bitcast.123), calls=%async_computation.1 | async-start | bytes 4194304 | tf_op jit(solution)/shard_map/all_to_all | solution.py:81
  66.1 53.0 %all-gather.2.cloned.1.call-start = ((), (), s32[]{:S(2)}) async-start(), calls=%async_computation.8 | async-start | bytes 3145728 | tf_op jit(solution)/shard_map/all_gather | solution.py:17
  113.2 37.8 %all-to-all-start.3 = ((bf16[32,16,1024]{2,0,1:T(8,128)(2,1)}), bf16[32,16,1024]{2,0,1:T(8,128)(2,1)}, u32[]{:S(2)}, u32[]{:S(2)}) async-start(bf16[32,16,1024]{2,0,1:T(8,128)(2,1)} %bitcast.126), calls=%async_computation.3 | async-start | bytes 2097152 | tf_op jit(solution)/shard_map/all_to_all | solution.py:84
  118.3 3.4 copy-start.6
  118.3 32.7 %all-reduce.2.cloned.1.call-start = ((), (), s32[]{:S(2)}) async-start(), calls=%async_computation.9 | async-start | bytes 1048576 | tf_op jit(solution)/shard_map/psum | solution.py:96
  121.7 29.3 %copy-start.7 = (f32[512]{0:T(512)S(1)}, f32[512]{0:T(512)}, u32[]{:S(2)}) copy-start(f32[512]{0:T(512)} %param.7) | copy-start | bytes 6148
  157.3 1.3 copy-start.1
  160.6 4.3 copy-start
  196.7 53.3 %all-to-all-start.6 = ((f32[16,1,32768]{2,1,0:T(1,128)}), f32[16,1,32768]{2,1,0:T(1,128)}, u32[]{:S(2)}, u32[]{:S(2)}) async-start(f32[16,1,32768]{2,1,0:T(1,128)} %reshape.100), calls=%async_computation.6 | async-start | bytes 4194304 | tf_op jit(solution)/shard_map/all_to_all | solution.py:118
  250.0 52.5 %all-to-all-start.4 = ((f32[16,1,32768]{2,1,0:T(1,128)}), f32[16,1,32768]{2,1,0:T(1,128)}, u32[]{:S(2)}, u32[]{:S(2)}) async-start(f32[16,1,32768]{2,1,0:T(1,128)} %reshape.96), calls=%async_computation.4 | async-start | bytes 4194304 | tf_op jit(solution)/shard_map/all_to_all | solution.py:109
  302.5 38.2 %all-to-all-start.7 = ((f32[2,1,262144]{2,1,0:T(1,128)}), f32[2,1,262144]{2,1,0:T(1,128)}, u32[]{:S(2)}, u32[]{:S(2)}) async-start(f32[2,1,262144]{2,1,0:T(1,128)} %reshape.102), calls=%async_computation.7 | async-start | bytes 4194304 | tf_op jit(solution)/shard_map/all_to_all | solution.py:117
  340.7 30.6 %all-to-all-start.5 = ((f32[2,1,262144]{2,1,0:T(1,128)}), f32[2,1,262144]{2,1,0:T(1,128)}, u32[]{:S(2)}, u32[]{:S(2)}) async-start(f32[2,1,262144]{2,1,0:T(1,128)} %reshape.98), calls=%async_computation.5 | async-start | bytes 4194304 | tf_op jit(solution)/shard_map/all_to_all | solution.py:108
  386.0 14.1 %slice-start = ((s8[8388608]{0:T(1024)(128)(4,1)}), s8[4194304]{0:T(1024)(128)(4,1)S(1)}, s32[]{:S(2)}) async-start(s8[8388608]{0:T(1024)(128)(4,1)} %bitcast.107), calls=%async_computation.10 | async-start | bytes 8388608
  390.6 9.5 %slice-start.1 = ((s8[8388608]{0:T(1024)(128)(4,1)}), s8[4194304]{0:T(1024)(128)(4,1)S(1)}, s32[]{:S(2)}) async-start(s8[8388608]{0:T(1024)(128)(4,1)} %bitcast.107), calls=%async_computation.11 | async-start | bytes 8388608
Sparse Core Ops, SparseCore 0:
  69.0 33.9 all-gather.1
  121.4 29.5 all-reduce.1
